TPU v7x, 32 devices: a whole 2x2x4 slice. The times are simulated.
32 devices in a mesh: seq: 16 (over z, x, core), head: 2 (over y).
Axes of the slice: x: 2, y: 2, z: 4, core: 2. Of those that a mesh axis runs over, the one named last changes fastest.
Arguments:
- x_proj: bfloat16 [4096, 8192], P(('seq', 'head')), may hold values from -6 to 6
- z_proj: bfloat16 [4096, 8192], P(('seq', 'head')), may hold values from -6 to 6
- b_proj: bfloat16 [4096, 1024], P(('seq', 'head')), may hold values from -6 to 6
- c_proj: bfloat16 [4096, 1024], P(('seq', 'head')), may hold values from -6 to 6
- dt_raw: bfloat16 [4096, 128], P(('seq', 'head')), may hold values from -3.2 to 3.2, as said below
- dt_bias: float32 [128], P('head'), may hold values from -6.3 to -1.2, as said below
- a_log: float32 [128], P('head'), as said below
- d_skip: float32 [128], P('head'), may hold values from 0.5 to 2
- conv_x: float32 [4, 8192], P(None, 'head'), may hold values from -3 to 3
- conv_bias_x: float32 [8192], P('head'), may hold values from -3 to 3
- conv_bc: float32 [4, 2, 1024], P(None, None, 'head'), may hold values from -3 to 3
- conv_bias_bc: float32 [2, 1024], P(None, 'head'), may hold values from -3 to 3
- norm_weight: float32 [8192], P('head'), may hold values from 0.25 to 1.75
- out_weight: bfloat16 [8192, 4096], P('head', 'seq'), may hold values from -0.0625 to 0.0625
Outputs:
- mixed: bfloat16 [4096, 4096], P(('seq', 'head'))
Inputs may be any that keep to these rules, and one draw needn't show every extreme that they name: `dt_raw`: A normal draw times 0.7 plus an offset common to each head and each aligned run of 256 tokens. `dt_bias`: the inverse softplus of a per-head step size between 0.002 and 0.25. Finite; exp(a_log) lies above 0.0 and at most 0.3.
All inputs are finite; a program needn't handle non-finite values.
Results may differ from a plain program's by a relative error of at most 0.014.
Values may be sent and summed in bfloat16 or wider, within the bound.
A program may use at most 192 MiB of HBM per device.

v0:
```python
import jax
import jax.numpy as jnp
from jax import lax
from jax.sharding import PartitionSpec as P

HEAD_DIM = 64
STATE = 128
GROUPS = 8
SPAN = 128
DI = 8192


def from_behind(array, axis, by):
    count = lax.axis_size(axis)
    pairs = [(i, i + by) for i in range(count) if 0 <= i + by < count]
    return lax.ppermute(array, axis, pairs)


def prefix(value, axis, join, neutral):
    count, mine = (lax.axis_size(axis), lax.axis_index(axis))
    pieces = jax.tree.map(lambda part: lax.all_gather(part, axis), value)
    total = jax.tree.map(
        lambda part, zero: jnp.full_like(part, 0) + jnp.asarray(zero, part.dtype), value, neutral
    )

    def lap(position, total):
        longer = join(total, jax.tree.map(lambda part: part[position], pieces))
        return jax.tree.map(lambda new, old: jnp.where(position < mine, new, old), longer, total)

    return lax.fori_loop(0, count - 1, lap, total)


def depthwise(current, previous, weight, bias_row):
    padded = jnp.concatenate([previous, current], axis=0).astype(jnp.float32)
    token_count = current.shape[0]
    summed = jnp.broadcast_to(bias_row, current.shape)
    for offset in range(weight.shape[0]):
        summed = summed + weight[offset] * padded[offset : offset + token_count]
    return jax.nn.silu(summed).astype(jnp.bfloat16)


def block_weights(c_blocks, b_blocks, cumulative, step_size, per_group):
    scores = jnp.einsum("ktgn,ksgn->kgts", c_blocks, b_blocks, preferred_element_type=jnp.float32)
    by_head = jnp.transpose(cumulative, (0, 2, 1))
    spread = by_head[:, :, :, None] - by_head[:, :, None, :]
    length = cumulative.shape[1]
    causal = jnp.arange(length)[:, None] >= jnp.arange(length)[None, :]
    decays = jnp.exp(jnp.where(causal, spread, -jnp.inf))
    scaled = decays * jnp.transpose(step_size, (0, 2, 1))[:, :, None, :]
    block_count = cumulative.shape[0]
    head_count = cumulative.shape[2]
    grouped = scaled.reshape(block_count, -1, per_group, length, length) * scores[:, :, None]
    return grouped.reshape(block_count, head_count, length, length).astype(jnp.bfloat16)


def combine_states(earlier, later):
    return (earlier[0] + later[0], jnp.exp(later[0])[:, None, None] * earlier[1] + later[1])


def per_device(
    x_proj,
    z_proj,
    b_proj,
    c_proj,
    dt_raw,
    dt_bias,
    a_log,
    d_skip,
    conv_x,
    conv_bias_x,
    conv_bc,
    conv_bias_bc,
    norm_weight,
    out_weight,
):
    x_heads, z_heads, b_heads, c_heads, dt_heads = (
        lax.all_to_all(x_proj, "head", split_axis=1, concat_axis=0, tiled=True),
        lax.all_to_all(z_proj, "head", split_axis=1, concat_axis=0, tiled=True),
        lax.all_to_all(b_proj, "head", split_axis=1, concat_axis=0, tiled=True),
        lax.all_to_all(c_proj, "head", split_axis=1, concat_axis=0, tiled=True),
        lax.all_to_all(dt_raw, "head", split_axis=1, concat_axis=0, tiled=True),
    )
    kernel_len = conv_x.shape[0]
    x_cols = x_heads.shape[1]
    bc_cols = b_heads.shape[1]
    last_rows = jnp.concatenate(
        [x_heads[-(kernel_len - 1) :], b_heads[-(kernel_len - 1) :], c_heads[-(kernel_len - 1) :]],
        axis=1,
    )
    before = from_behind(last_rows, "seq", 1)
    x_conv = depthwise(x_heads, before[:, :x_cols], conv_x, conv_bias_x)
    b_conv = depthwise(
        b_heads, before[:, x_cols : x_cols + bc_cols], conv_bc[:, 0], conv_bias_bc[0]
    )
    c_conv = depthwise(c_heads, before[:, x_cols + bc_cols :], conv_bc[:, 1], conv_bias_bc[1])
    token_count = x_conv.shape[0]
    local_heads = dt_bias.shape[0]
    local_groups = bc_cols // STATE
    per_group = local_heads // local_groups
    blocks = token_count // SPAN
    x_blocks = x_conv.reshape(blocks, SPAN, local_heads, HEAD_DIM)
    b_blocks = b_conv.reshape(blocks, SPAN, local_groups, STATE)
    c_blocks = c_conv.reshape(blocks, SPAN, local_groups, STATE)
    step_size = jax.nn.softplus(dt_heads.astype(jnp.float32) + dt_bias).reshape(
        blocks, SPAN, local_heads
    )
    cumulative = jnp.cumsum(-jnp.exp(a_log) * step_size, axis=1)
    mix_weights = block_weights(c_blocks, b_blocks, cumulative, step_size, per_group)
    y_local = jnp.einsum(
        "khts,kshp->kthp", mix_weights, x_blocks, preferred_element_type=jnp.float32
    )
    state_scale = step_size * jnp.exp(cumulative[:, -1:, :] - cumulative)
    x_weighted = (x_blocks.astype(jnp.float32) * state_scale[:, :, :, None]).astype(jnp.bfloat16)
    x_grouped = x_weighted.reshape(blocks, SPAN, local_groups, per_group, HEAD_DIM)
    pieces = jnp.einsum(
        "ksgqp,ksgn->kgqpn", x_grouped, b_blocks, preferred_element_type=jnp.float32
    )
    pieces = pieces.reshape(blocks, local_heads, HEAD_DIM, STATE)
    totals = cumulative[:, -1, :]
    final_state = jnp.zeros((local_heads, HEAD_DIM, STATE), jnp.float32)
    for block_idx in range(blocks):
        final_state = jnp.exp(totals[block_idx])[:, None, None] * final_state + pieces[block_idx]
    log_total = jnp.sum(totals, axis=0)
    carried = prefix(
        (log_total, final_state),
        "seq",
        combine_states,
        (jnp.zeros_like(log_total), jnp.zeros_like(final_state)),
    )
    running = carried[1]
    start_list = []
    for block_idx in range(blocks):
        start_list.append(running.astype(jnp.bfloat16))
        running = jnp.exp(totals[block_idx])[:, None, None] * running + pieces[block_idx]
    start_states = jnp.stack(start_list).reshape(blocks, local_groups, per_group, HEAD_DIM, STATE)
    y_carry = jnp.einsum(
        "ktgn,kgqpn->ktgqp", c_blocks, start_states, preferred_element_type=jnp.float32
    )
    y_carry = (
        y_carry.reshape(blocks, SPAN, local_heads, HEAD_DIM) * jnp.exp(cumulative)[:, :, :, None]
    )
    outputs = y_local + y_carry + d_skip[:, None] * x_blocks.astype(jnp.float32)
    outputs = outputs.reshape(token_count, local_heads * HEAD_DIM)
    gated = outputs * jax.nn.silu(z_heads.astype(jnp.float32))
    grouped = gated.reshape(token_count, -1, DI // GROUPS)
    normed = grouped / jnp.sqrt(jnp.mean(grouped * grouped, axis=-1, keepdims=True) + 1.0)
    normed = (normed.reshape(token_count, -1) * norm_weight).astype(jnp.bfloat16)
    terms = jnp.dot(
        normed,
        lax.all_gather(out_weight, "seq", axis=1, tiled=True),
        preferred_element_type=jnp.float32,
    )
    mixed = lax.psum_scatter(terms.astype(jnp.bfloat16), "head", scatter_dimension=0, tiled=True)
    return mixed


def solution(mesh):
    in_specs = (
        P(("seq", "head"), None),
        P(("seq", "head"), None),
        P(("seq", "head"), None),
        P(("seq", "head"), None),
        P(("seq", "head"), None),
        P("head"),
        P("head"),
        P("head"),
        P(None, "head"),
        P("head"),
        P(None, None, "head"),
        P(None, "head"),
        P("head"),
        P("head", "seq"),
    )
    out_specs = P(("seq", "head"), None)
    return jax.shard_map(
        per_device, mesh=mesh, in_specs=in_specs, out_specs=out_specs, check_vma=False
    )
```

profile of v0, /device:TPU:0, one launch (start us, length us, event | category | flops | bytes accessed | tf_op | source)
XLA Modules:
  0.0 497.7 jit_solution(14551310706796745205)
XLA Ops:
  8.1 4.3 all-to-all-start.3
  14.0 4.1 copy.68
  19.8 3.4 all-to-all-start.1
  23.9 5.1 %all-to-all-done.1 = bf16[128,2,512]{0,2,1:T(8,128)(2,1)S(1)} async-done(((bf16[128,2,512]{0,2,1:T(8,128)(2,1)}), bf16[128,2,512]{0,2,1:T(8,128)(2,1)S(1)}, u32[]{:S(2)}, u32[]{:S(2)}) %all-to-all-start.1) | async-done | bytes 262176 | tf_op jit(solution)/shard_map/all_to_all | solution.py:79
  28.9 3.4 all-to-all-start.2
  33.0 4.6 all-to-all-done.2
  37.6 3.8 all-to-all-start
  43.4 21.3 %all-to-all-done = bf16[128,2,4096]{0,2,1:T(8,128)(2,1)S(1)} async-done(((bf16[128,2,4096]{0,2,1:T(8,128)(2,1)}), bf16[128,2,4096]{0,2,1:T(8,128)(2,1)S(1)}, u32[]{:S(2)}, u32[]{:S(2)}) %all-to-all-start) | async-done | bytes 2097184 | tf_op jit(solution)/shard_map/all_to_all | solution.py:77
  66.0 2.9 copy.69
  74.5 2.7 multiply_convert_fusion.4
  77.3 3.1 copy.83
  80.4 5.8 %reshape.168 = f32[2,128,4,16,64]{1,0,4,3,2:T(2,128)} reshape(f32[256,4096]{0,1:T(8,128)} %copy.83) | data formatting | bytes 8388608 | tf_op jit(solution)/shard_map/convert_element_type | solution.py:113
  86.2 4.5 multiply_convert_fusion.3
  95.8 2.5 copy.92
  98.3 4.8 all-to-all-start.4
  105.3 36.4 %all-reduce = f32[1024]{0:T(1024)S(1)} all-reduce(f32[1024]{0:T(1024)S(1)} %dynamic-update-slice), channel_id=2, replica_groups=mesh['seq'=16,'head'=2] {'seq'}, use_global_device_ids=true, to_apply=%add | all-reduce | flops 1024 | bytes 8192
  143.4 3.9 convert_bitcast_fusion
  147.2 5.8 %copy.93 = f32[2,128,4096]{2,1,0:T(8,128)} copy(f32[2,128,4096]{1,2,0:T(8,128)} %convert_bitcast_fusion) | data formatting | bytes 8388608 | tf_op jit(solution)/shard_map/convert_element_type | solution.py:144
  153.1 7.0 %reshape.180 = bf16[2,128,64,64]{3,2,1,0:T(8,128)(2,1)} reshape(bf16[256,4096]{1,0:T(8,128)(2,1)} %copy-done.1) | data formatting | bytes 4194304 | tf_op jit(solution)/shard_map/reshape | solution.py:101
  160.5 6.6 %copy.82 = bf16[2,128,64,64]{1,3,2,0:T(8,128)(2,1)} copy(bf16[2,128,64,64]{3,2,1,0:T(8,128)(2,1)} %reshape.180) | data formatting | bytes 4194304 | tf_op jit(solution)/shard_map/reshape | solution.py:101
  167.4 99.6 %all-gather.4.cloned.1.call-done = f32[16,64,64,128]{3,2,1,0:T(8,128)} async-done(((f32[1,64,64,128]{3,2,1,0:T(8,128)}), f32[16,64,64,128]{3,2,1,0:T(8,128)}) %all-gather.4.cloned.1.call-update) | async-done | bytes 33554448 | tf_op jit(solution)/shard_map/all_gather | solution.py:21
  267.0 42.3 %while.14 = (s32[]{:T(128)}, f32[64,64,128]{2,1,0:T(8,128)S(1)}, s32[]{:T(128)}, f32[16,64]{1,0:T(8,128)}, f32[16,64,64,128]{3,2,1,0:T(8,128)}, /*index=5*/s32[]{:T(128)}, s32[]{:T(128)}) while((s32[]{:T(128)}, f32[64,64,128]{2,1,0:T(8,128)S(1)}, s32[]{:T(128)}, f32[16,64]{1,0:T(8,128)}, f32[16,64,64,128]{3,2,1,0:T(8,128)}, ...), condition=%wide.region_3.4_spmd.clone, body=%wide.region_2.3_spmd.clone.sunk | while | flops 2097156 | bytes 6292329 | solution.py:30
  276.0 2.1 fusion.61
  301.3 2.3 fusion.61
  309.4 2.1 fusion.51
  313.8 8.7 %multiply_reduce_fusion = (f32[2,128,64]{1,2,0:T(8,128)S(1)}, f32[2,128,64,64]{1,3,2,0:T(8,128)}) fusion(bf16[128,2,4096]{0,2,1:T(8,128)(2,1)} %all-to-all-done.4, bf16[2,128,64,64]{1,3,2,0:T(8,128)(2,1)S(1)} %copy-done.5, f32[64]{0:T(128)S(1)} %copy-done.32, f32[2,128,64,64]{1,3,2,0:T(8,128)S(1)} %bitcast.142, f32[2,128,64]{1,2,0:T(8,128)S(1)} %copy.89, ...), kind=kOutput, calls=%fused_computation.24 | convolution fusion | flops 292536320 | bytes 21250304 | tf_op jit(solution)/shard_map/khts,kshp->kthp/dot_general | solution.py:109
  322.5 9.2 %copy.103 = f32[2,128,64,64]{3,2,1,0:T(8,128)} copy(f32[2,128,64,64]{1,3,2,0:T(8,128)} %get-tuple-element.155) | data formatting | bytes 8388608 | tf_op jit(solution)/shard_map/reshape | solution.py:143
  331.7 8.0 %reshape.179 = f32[256,4096]{1,0:T(8,128)} reshape(f32[2,128,64,64]{3,2,1,0:T(8,128)} %copy.103) | data formatting | bytes 8388608 | tf_op jit(solution)/shard_map/reshape | solution.py:143
  340.6 3.9 copy.107
  346.4 98.2 %all-gather.6.cloned.1.call-done = bf16[4096,4096]{1,0:T(8,128)(2,1)} async-done(((bf16[4096,256]{1,0:T(8,128)(2,1)}), bf16[4096,4096]{1,0:T(8,128)(2,1)}) %all-gather.6.cloned.1.call-update) | async-done | bytes 33554448 | tf_op jit(solution)/shard_map/all_gather | solution.py:150
  444.6 16.6 %convolution_convert_fusion = bf16[256,4096]{1,0:T(8,128)(2,1)} fusion(bf16[256,4096]{1,0:T(8,128)(2,1)S(1)} %multiply_convert_fusion.2, bf16[4096,4096]{1,0:T(8,128)(2,1)} %all-gather.6.cloned.1.call-done), kind=kOutput, calls=%fused_computation.4 | convolution fusion | flops 8590983168 | bytes 37748736 | tf_op jit(solution)/shard_map/dot_general | solution.py:148
  461.3 29.9 %reduce-scatter.2.cloned.1.call-done = bf16[128,4096]{1,0:T(8,128)(2,1)} async-done(((bf16[256,4096]{1,0:T(8,128)(2,1)}), bf16[128,4096]{1,0:T(8,128)(2,1)}) %reduce-scatter.2.cloned.1.call-update) | async-done | bytes 1048592 | tf_op jit(solution)/shard_map/reduce_scatter | solution.py:153
  (159 shorter events, 66.3 us)
Async XLA Ops:
  6.5 11.6 %copy-start.7 = (bf16[128,1024]{1,0:T(8,128)(2,1)S(1)}, bf16[128,1024]{1,0:T(8,128)(2,1)}, u32[]{:S(2)}) copy-start(bf16[128,1024]{1,0:T(8,128)(2,1)} %param.18) | copy-start | bytes 786436
  6.5 12.4 %copy-start.8 = (bf16[128,1024]{1,0:T(8,128)(2,1)S(1)}, bf16[128,1024]{1,0:T(8,128)(2,1)}, u32[]{:S(2)}) copy-start(bf16[128,1024]{1,0:T(8,128)(2,1)} %param.19) | copy-start | bytes 786436
  6.5 16.7 %copy-start.15 = (f32[4,2,512]{2,1,0:T(2,128)S(1)}, f32[4,2,512]{2,1,0:T(2,128)}, u32[]{:S(2)}) copy-start(f32[4,2,512]{2,1,0:T(2,128)} %param.26) | copy-start | bytes 49156
  6.5 25.9 %copy-start.26 = (f32[2,512]{1,0:T(2,128)S(1)}, f32[2,512]{1,0:T(2,128)}, u32[]{:S(2)}) copy-start(f32[2,512]{1,0:T(2,128)} %param.27) | copy-start | bytes 12292
  8.1 11.7 %all-to-all-start.3 = ((bf16[128,2,64]{0,2,1:T(8,128)(2,1)}), bf16[128,2,64]{0,2,1:T(8,128)(2,1)S(1)}, u32[]{:S(2)}, u32[]{:S(2)}) async-start(bf16[128,2,64]{0,2,1:T(8,128)(2,1)} %bitcast.13), calls=%async_computation.3 | async-start | bytes 65536 | tf_op jit(solution)/shard_map/all_to_all | solution.py:81
  18.1 23.3 %copy-start.31 = (f32[64]{0:T(128)S(1)}, f32[64]{0:T(128)}, u32[]{:S(2)}) copy-start(f32[64]{0:T(128)} %param.22) | copy-start | bytes 772
  18.1 23.4 %copy-start.24 = (f32[64]{0:T(128)S(1)}, f32[64]{0:T(128)}, u32[]{:S(2)}) copy-start(f32[64]{0:T(128)} %param.21) | copy-start | bytes 772
  19.8 9.1 %all-to-all-start.1 = ((bf16[128,2,512]{0,2,1:T(8,128)(2,1)}), bf16[128,2,512]{0,2,1:T(8,128)(2,1)S(1)}, u32[]{:S(2)}, u32[]{:S(2)}) async-start(bf16[128,2,512]{0,2,1:T(8,128)(2,1)} %bitcast.4), calls=%async_computation.1 | async-start | bytes 524288 | tf_op jit(solution)/shard_map/all_to_all | solution.py:79
  28.9 8.6 %all-to-all-start.2 = ((bf16[128,2,512]{0,2,1:T(8,128)(2,1)}), bf16[128,2,512]{0,2,1:T(8,128)(2,1)S(1)}, u32[]{:S(2)}, u32[]{:S(2)}) async-start(bf16[128,2,512]{0,2,1:T(8,128)(2,1)} %bitcast.7), calls=%async_computation.2 | async-start | bytes 524288 | tf_op jit(solution)/shard_map/all_to_all | solution.py:80
  37.6 27.1 %all-to-all-start = ((bf16[128,2,4096]{0,2,1:T(8,128)(2,1)}), bf16[128,2,4096]{0,2,1:T(8,128)(2,1)S(1)}, u32[]{:S(2)}, u32[]{:S(2)}) async-start(bf16[128,2,4096]{0,2,1:T(8,128)(2,1)} %bitcast.1), calls=%async_computation | async-start | bytes 4194304 | tf_op jit(solution)/shard_map/all_to_all | solution.py:77
  41.3 225.7 %all-gather.4.cloned.1.call-start = ((), (), s32[]{:S(2)}) async-start(), calls=%async_computation.6 | async-start | bytes 35651584 | tf_op jit(solution)/shard_map/all_gather | solution.py:21
  69.0 2.2 collective-permute-start
  77.3 8.9 %copy-start.1 = (bf16[256,4096]{1,0:T(8,128)(2,1)}, bf16[256,4096]{1,0:T(8,128)(2,1)S(1)}, u32[]{:S(2)}) copy-start(bf16[256,4096]{1,0:T(8,128)(2,1)S(1)} %multiply_convert_fusion.4) | copy-start | bytes 6291460
  91.4 1.9 copy-start.28
  91.4 1.9 copy-start.30
  93.4 2.4 copy-start.6
  95.0 349.6 %all-gather.6.cloned.1.call-start = ((), (), s32[]{:S(2)}) async-start(), calls=%async_computation.7 | async-start | bytes 35651584 | tf_op jit(solution)/shard_map/all_gather | solution.py:150
  95.8 7.4 %copy-start.33 = (u32[32]{0:T(128)S(1)}, u32[32]{0:T(128)}, u32[]{:S(2)}) copy-start(u32[32]{0:T(128)} %constant.53) | copy-start | bytes 388
  95.8 9.3 %copy-start.29 = (f32[64]{0:T(128)S(1)}, f32[64]{0:T(128)}, u32[]{:S(2)}) copy-start(f32[64]{0:T(128)} %get-tuple-element.136) | copy-start | bytes 772
  95.8 46.7 %copy-start.25 = (f32[64]{0:T(128)S(1)}, f32[64]{0:T(128)}, u32[]{:S(2)}) copy-start(f32[64]{0:T(128)} %param.21) | copy-start | bytes 772
  98.3 45.0 %all-to-all-start.4 = ((bf16[128,2,4096]{0,2,1:T(8,128)(2,1)}), bf16[128,2,4096]{0,2,1:T(8,128)(2,1)}, u32[]{:S(2)}, u32[]{:S(2)}) async-start(bf16[128,2,4096]{0,2,1:T(8,128)(2,1)} %bitcast.43), calls=%async_computation.4 | async-start | bytes 4194304 | tf_op jit(solution)/shard_map/all_to_all | solution.py:78
  103.2 388.0 %reduce-scatter.2.cloned.1.call-start = ((), (), s32[]{:S(2)}) async-start(), calls=%async_computation.8 | async-start | bytes 3145728 | tf_op jit(solution)/shard_map/reduce_scatter | solution.py:153
  153.1 7.0 %copy-start.19 = (f32[1,1,512]{2,1,0:T(1,128)S(1)}, f32[1,1,512]{2,1,0:T(1,128)}, u32[]{:S(2)}) copy-start(f32[1,1,512]{2,1,0:T(1,128)} %get-tuple-element.144) | copy-start | bytes 6148
  153.1 7.0 %copy-start.20 = (f32[1,1,512]{2,1,0:T(1,128)S(1)}, f32[1,1,512]{2,1,0:T(1,128)}, u32[]{:S(2)}) copy-start(f32[1,1,512]{2,1,0:T(1,128)} %get-tuple-element.147) | copy-start | bytes 6148
  153.1 7.0 %copy-start.21 = (f32[1,1,512]{2,1,0:T(1,128)S(1)}, f32[1,1,512]{2,1,0:T(1,128)}, u32[]{:S(2)}) copy-start(f32[1,1,512]{2,1,0:T(1,128)} %get-tuple-element.148) | copy-start | bytes 6148
  153.1 7.0 %copy-start.22 = (f32[1,1,512]{2,1,0:T(1,128)S(1)}, f32[1,1,512]{2,1,0:T(1,128)}, u32[]{:S(2)}) copy-start(f32[1,1,512]{2,1,0:T(1,128)} %get-tuple-element.149) | copy-start | bytes 6148
  153.1 7.0 %copy-start.23 = (f32[1,512]{1,0:T(1,128)S(1)}, f32[1,512]{1,0:T(1,128)}, u32[]{:S(2)}) copy-start(f32[1,512]{1,0:T(1,128)} %get-tuple-element.152) | copy-start | bytes 6148
  267.0 42.4 %copy-start.27 = (f32[64]{0:T(128)S(1)}, f32[64]{0:T(128)}, u32[]{:S(2)}) copy-start(f32[64]{0:T(128)} %get-tuple-element.134) | copy-start | bytes 772
  312.2 1.6 copy-start.5
  339.9 4.6 copy-start.18
  340.6 4.0 copy-start.2
  340.6 4.0 copy-start.3
  (11 other events, 15.4 us)
Sparse Core Ops, SparseCore 0:
  95.2 171.7 all-gather.3
  268.5 176.0 all-gather.5
  461.4 29.7 reduce-scatter.1
where the time goes:
time: 500 us; the launch traced here: 498 us
  waiting for transfers between devices  260 us (52%)
  local copies, waits for them, and re-layouts  86 us (17%)
  other arithmetic  52.8 us (11%)
  blocking collectives  36.4 us (7%)
  matrix products  27 us (5%)
  starting transfers between devices  21.2 us (4%)
  between operations  14.4 us (3%)
    all_gather x1, waiting for transfers between devices, prefix(): pieces = jax.tree.map(lambda part: lax.all_gather(part, axis), value)  99.6 us
    all_gather x1, waiting for transfers between devices, per_device(): lax.all_gather(out_weight, 'seq', axis=1, tiled=True)  98.2 us
    unnamed x1, blocking collectives  36.4 us
    select_n x15, other arithmetic, lap(): jnp.where(position < mine, new, old)  31.7 us
    reduce_scatter x1, waiting for transfers between devices, per_device(): lax.psum_scatter(terms.astype(jnp.bfloat16), 'head', scatter_dimension=0,...  29.9 us
    all_to_all x1, waiting for transfers between devices, per_device(): lax.all_to_all(x_proj, 'head', split_axis=1, concat_axis=0, tiled=True)  21.3 us
    unnamed x77, local copies, waits for them, and re-layouts  18.4 us
    reshape x2, local copies, waits for them, and re-layouts, per_device(): outputs = outputs.reshape(token_count, local_heads * HEAD_DIM)  17.2 us
  transfers between devices with their start and end apart: 9, of which 7 were waited for; matrix products, arithmetic and copies ran while one was open for 24% of the time, Pallas kernels for 0%

commit v1 on v0

--- a/solution.py
+++ b/solution.py
@@ -147,7 +147,7 @@
     normed = (normed.reshape(token_count, -1) * norm_weight).astype(jnp.bfloat16)
     terms = jnp.dot(
         normed,
-        lax.all_gather(out_weight, "seq", axis=1, tiled=True),
+        jnp.concatenate(lax.all_gather(out_weight, "seq"), axis=1),
         preferred_element_type=jnp.float32,
     )
     mixed = lax.psum_scatter(terms.astype(jnp.bfloat16), "head", scatter_dimension=0, tiled=True)

time: 500 us -> 469 us (0.938)
  waiting for transfers between devices: 260 us -> 195 us
  local copies, waits for them, and re-layouts: 86 us -> 120 us
    all_gather x1, waiting for transfers between devices: 98.2 us -> 1.03 us  [per_device(): lax.all_gather(out_weight, 'seq')]
    reshape x0 -> x1, local copies, waits for them, and re-layouts: none -> 40.8 us  [per_device(): jnp.concatenate(lax.all_gather(out_weight, 'seq'), axis=1)]
    all_gather x1, waiting for transfers between devices: 99.6 us -> 130 us  [prefix(): pieces = jax.tree.map(lambda part: lax.all_gather(part, axis), value)]
    convert_element_type x1 -> x3, local copies, waits for them, and re-layouts: 5.81 us -> 17.2 us  [per_device(): gated = outputs * jax.nn.silu(z_heads.astype(jnp.float32))]
    reshape x2 -> x1, local copies, waits for them, and re-layouts: 17.2 us -> 6.45 us  [per_device(): outputs = outputs.reshape(token_count, local_heads * HEAD_DIM)]
    exp x15, local copies, waits for them, and re-layouts: 10.3 us -> 0.17 us  [combine_states(): jnp.exp(later[0])[:, None, None] * earlier[1] + later[1]]
    add x0 -> x1, local copies, waits for them, and re-layouts: none -> 5.86 us  [per_device(): outputs = y_local + y_carry + d_skip[:, None] * x_blocks.astype(jnp.float32)]
    unnamed x77 -> x69, local copies, waits for them, and re-layouts: 18.4 us -> 13.3 us
  transfers between devices with their start and end apart: 9 -> 9, of which waited for: 7 -> 7; matrix products, arithmetic and copies ran while one was open for 24% -> 25% of each run, Pallas kernels for 0% -> 0%
where the time goes in v1:
time: 469 us; the launch traced here: 466 us
  waiting for transfers between devices  195 us (42%)
  local copies, waits for them, and re-layouts  120 us (26%)
  other arithmetic  54.4 us (12%)
  blocking collectives  36 us (8%)
  matrix products  24.7 us (5%)
  starting transfers between devices  21.2 us (5%)
  between operations  14.3 us (3%)
    all_gather x1, waiting for transfers between devices, prefix(): pieces = jax.tree.map(lambda part: lax.all_gather(part, axis), value)  130 us
    reshape x1, local copies, waits for them, and re-layouts, per_device(): jnp.concatenate(lax.all_gather(out_weight, 'seq'), axis=1)  40.8 us
    unnamed x1, blocking collectives  36 us
    reduce_scatter x1, waiting for transfers between devices, per_device(): lax.psum_scatter(terms.astype(jnp.bfloat16), 'head', scatter_dimension=0,...  32.1 us
    select_n x15, other arithmetic, lap(): jnp.where(position < mine, new, old)  31.2 us
    all_to_all x1, waiting for transfers between devices, per_device(): lax.all_to_all(x_proj, 'head', split_axis=1, concat_axis=0, tiled=True)  21.8 us
    convert_element_type x3, local copies, waits for them, and re-layouts, per_device(): gated = outputs * jax.nn.silu(z_heads.astype(jnp.float32))  17.2 us
    dot_general x1, matrix products, per_device(): jnp.dot(normed, jnp.concatenate(lax.all_gather(out_weight, 'seq'), axis=1...  16 us
  transfers between devices with their start and end apart: 9, of which 7 were waited for; matrix products, arithmetic and copies ran while one was open for 25% of the time, Pallas kernels for 0%

profile of v1, /device:TPU:0, one launch (start us, length us, event | category | flops | bytes accessed | tf_op | source)
XLA Modules:
  0.0 465.7 jit_solution(11303701504898319845)
XLA Ops:
  8.7 4.3 all-to-all-start.3
  14.7 4.1 copy.72
  20.5 3.4 all-to-all-start.1
  24.5 5.0 %all-to-all-done.1 = bf16[128,2,512]{0,2,1:T(8,128)(2,1)S(1)} async-done(((bf16[128,2,512]{0,2,1:T(8,128)(2,1)}), bf16[128,2,512]{0,2,1:T(8,128)(2,1)S(1)}, u32[]{:S(2)}, u32[]{:S(2)}) %all-to-all-start.1) | async-done | bytes 262176 | tf_op jit(solution)/shard_map/all_to_all | solution.py:79
  29.6 3.4 all-to-all-start.2
  33.6 4.5 all-to-all-done.2
  38.2 3.8 all-to-all-start
  44.1 21.8 %all-to-all-done = bf16[128,2,4096]{0,2,1:T(8,128)(2,1)S(1)} async-done(((bf16[128,2,4096]{0,2,1:T(8,128)(2,1)}), bf16[128,2,4096]{0,2,1:T(8,128)(2,1)S(1)}, u32[]{:S(2)}, u32[]{:S(2)}) %all-to-all-start) | async-done | bytes 2097184 | tf_op jit(solution)/shard_map/all_to_all | solution.py:77
  67.2 2.9 copy.73
  75.8 2.7 multiply_convert_fusion.4
  78.5 3.1 copy.87
  81.6 5.8 %reshape.223 = f32[2,128,4,16,64]{1,0,4,3,2:T(2,128)} reshape(f32[256,4096]{0,1:T(8,128)} %copy.87) | data formatting | bytes 8388608 | tf_op jit(solution)/shard_map/convert_element_type | solution.py:113
  87.4 4.7 %multiply_convert_fusion.3 = bf16[2,128,4,16,64]{1,0,4,3,2:T(2,128)(2,1)S(1)} fusion(f32[2,128,4,16,64]{1,0,4,3,2:T(2,128)} %reshape.223, f32[2,128,4,16]{1,0,3,2:T(2,128)S(1)} %copy.89), kind=kLoop, calls=%fused_computation.19 | loop fusion | flops 2097152 | bytes 6356992 | tf_op jit(solution)/shard_map/convert_element_type | solution.py:113
  98.8 4.9 %all-to-all-start.4 = ((bf16[128,2,4096]{2,0,1:T(8,128)(2,1)}), bf16[128,2,4096]{2,0,1:T(8,128)(2,1)}, u32[]{:S(2)}, u32[]{:S(2)}) async-start(bf16[128,2,4096]{2,0,1:T(8,128)(2,1)} %bitcast.115), calls=%async_computation.4 | async-start | bytes 4194304 | tf_op jit(solution)/shard_map/all_to_all | solution.py:78
  105.3 36.0 %all-reduce = f32[1024]{0:T(1024)S(1)} all-reduce(f32[1024]{0:T(1024)S(1)} %dynamic-update-slice), channel_id=2, replica_groups=mesh['seq'=16,'head'=2] {'seq'}, use_global_device_ids=true, to_apply=%add | all-reduce | flops 1024 | bytes 8192
  143.5 4.1 convert_bitcast_fusion
  147.6 5.6 %copy.99 = f32[2,128,4096]{1,2,0:T(8,128)} copy(f32[2,128,4096]{2,1,0:T(8,128)} %convert_bitcast_fusion) | data formatting | bytes 8388608 | tf_op jit(solution)/shard_map/convert_element_type | solution.py:144
  153.2 6.2 %reshape.224 = f32[256,4,1024]{2,1,0:T(4,128)} reshape(f32[2,128,4096]{2,1,0:T(8,128)} %convert_bitcast_fusion) | data formatting | bytes 8388608 | tf_op jit(solution)/shard_map/convert_element_type | solution.py:144
  159.4 5.3 %copy.98 = f32[256,4,1024]{0,2,1:T(8,128)} copy(f32[256,4,1024]{2,1,0:T(4,128)} %reshape.224) | data formatting | bytes 8388608 | tf_op jit(solution)/shard_map/convert_element_type | solution.py:144
  164.8 6.9 %reshape.235 = bf16[2,128,64,64]{3,2,1,0:T(8,128)(2,1)} reshape(bf16[256,4096]{1,0:T(8,128)(2,1)} %copy-done.1) | data formatting | bytes 4194304 | tf_op jit(solution)/shard_map/reshape | solution.py:101
  172.2 6.5 %copy.86 = bf16[2,128,64,64]{1,3,2,0:T(8,128)(2,1)} copy(bf16[2,128,64,64]{3,2,1,0:T(8,128)(2,1)} %reshape.235) | data formatting | bytes 4194304 | tf_op jit(solution)/shard_map/reshape | solution.py:101
  180.0 40.8 %copy.101 = bf16[4096,16,256]{0,2,1:T(8,128)(2,1)} copy(bf16[4096,16,256]{2,0,1:T(8,128)(2,1)} %bitcast.120) | data formatting | bytes 67108864 | tf_op jit(solution)/shard_map/reshape | solution.py:150
  220.8 129.7 %all-gather.5.cloned.1.call-done = f32[16,64,64,128]{3,2,1,0:T(8,128)} async-done(((f32[1,64,64,128]{3,2,1,0:T(8,128)}), f32[16,64,64,128]{3,2,1,0:T(8,128)}) %all-gather.5.cloned.1.call-update) | async-done | bytes 33554448 | tf_op jit(solution)/shard_map/all_gather | solution.py:21
  350.5 31.8 %while.14 = (s32[]{:T(128)}, f32[64,64,128]{2,1,0:T(8,128)S(1)}, s32[]{:T(128)}, f32[16,64]{1,0:T(8,128)S(1)}, f32[16,64,64,128]{3,2,1,0:T(8,128)}, /*index=5*/s32[]{:T(128)}, s32[]{:T(128)}) while((s32[]{:T(128)}, f32[64,64,128]{2,1,0:T(8,128)S(1)}, s32[]{:T(128)}, f32[16,64]{1,0:T(8,128)S(1)}, f32[16,64,64,128]{3,2,1,0:T(8,128)}, ...), condition=%wide.region_3.4_spmd.clone, body=%wide.region_2.3_spmd.clone.sunk | while | flops 2097156 | bytes 6292329 | solution.py:30
  352.6 2.1 fusion.56
  382.4 2.1 fusion.46
  387.4 7.0 %multiply_reduce_fusion = (f32[2,128,64]{1,2,0:T(8,128)}, f32[2,128,64,64]{1,3,2,0:T(8,128)S(1)}) fusion(f32[2,128,4096]{1,2,0:T(8,128)S(1)} %copy-done.3, bf16[2,128,64,64]{1,3,2,0:T(8,128)(2,1)} %copy.86, f32[64]{0:T(128)S(1)} %copy-done.29, f32[2,128,64,64]{1,3,2,0:T(8,128)S(1)} %bitcast.130, f32[2,128,64]{1,2,0:T(8,128)} %copy.93, ...), kind=kOutput, calls=%fused_computation.18 | convolution fusion | flops 291487744 | bytes 23347456 | tf_op jit(solution)/shard_map/khts,kshp->kthp/dot_general | solution.py:109
  394.4 5.9 %copy.95 = f32[2,128,64,64]{1,0,3,2:T(2,128)} copy(f32[2,128,64,64]{1,3,2,0:T(8,128)S(1)} %get-tuple-element.155) | data formatting | bytes 8388608 | tf_op jit(solution)/shard_map/add | solution.py:142
  400.2 6.5 %reshape.220 = f32[256,4,1024]{0,2,1:T(8,128)} reshape(f32[2,128,64,64]{1,0,3,2:T(2,128)} %copy.95) | data formatting | bytes 8388608 | tf_op jit(solution)/shard_map/reshape | solution.py:143
  406.9 4.2 multiply_convert_fusion.2
  411.1 16.0 %convolution_convert_fusion = bf16[256,4096]{1,0:T(8,128)(2,1)} fusion(bf16[256,4096]{0,1:T(8,128)(2,1)S(1)} %bitcast.133, bf16[4096,4096]{0,1:T(8,128)(2,1)} %bitcast.121), kind=kOutput, calls=%fused_computation.4 | convolution fusion | flops 8590983168 | bytes 37748736 | tf_op jit(solution)/shard_map/dot_general | solution.py:148
  427.1 32.1 %reduce-scatter.2.cloned.1.call-done = bf16[128,4096]{1,0:T(8,128)(2,1)} async-done(((bf16[256,4096]{1,0:T(8,128)(2,1)}), bf16[128,4096]{1,0:T(8,128)(2,1)}) %reduce-scatter.2.cloned.1.call-update) | async-done | bytes 1048592 | tf_op jit(solution)/shard_map/reduce_scatter | solution.py:153
  (154 shorter events, 59.4 us)
Async XLA Ops:
  6.5 12.2 %copy-start.5 = (bf16[128,1024]{1,0:T(8,128)(2,1)S(1)}, bf16[128,1024]{1,0:T(8,128)(2,1)}, u32[]{:S(2)}) copy-start(bf16[128,1024]{1,0:T(8,128)(2,1)} %param.18) | copy-start | bytes 786436
  6.5 13.1 %copy-start.6 = (bf16[128,1024]{1,0:T(8,128)(2,1)S(1)}, bf16[128,1024]{1,0:T(8,128)(2,1)}, u32[]{:S(2)}) copy-start(bf16[128,1024]{1,0:T(8,128)(2,1)} %param.19) | copy-start | bytes 786436
  6.5 17.4 %copy-start.13 = (f32[4,2,512]{2,1,0:T(2,128)S(1)}, f32[4,2,512]{2,1,0:T(2,128)}, u32[]{:S(2)}) copy-start(f32[4,2,512]{2,1,0:T(2,128)} %param.26) | copy-start | bytes 49156
  6.5 26.5 %copy-start.23 = (f32[2,512]{1,0:T(2,128)S(1)}, f32[2,512]{1,0:T(2,128)}, u32[]{:S(2)}) copy-start(f32[2,512]{1,0:T(2,128)} %param.27) | copy-start | bytes 12292
  6.5 173.5 %all-gather.7.cloned.1.call-start = ((), (), s32[]{:S(2)}) async-start(), calls=%async_computation.8 | async-start | bytes 35651584 | tf_op jit(solution)/shard_map/all_gather | solution.py:150
  8.7 11.7 %all-to-all-start.3 = ((bf16[128,2,64]{0,2,1:T(8,128)(2,1)}), bf16[128,2,64]{0,2,1:T(8,128)(2,1)S(1)}, u32[]{:S(2)}, u32[]{:S(2)}) async-start(bf16[128,2,64]{0,2,1:T(8,128)(2,1)} %bitcast.13), calls=%async_computation.3 | async-start | bytes 65536 | tf_op jit(solution)/shard_map/all_to_all | solution.py:81
  18.8 23.3 %copy-start.28 = (f32[64]{0:T(128)S(1)}, f32[64]{0:T(128)}, u32[]{:S(2)}) copy-start(f32[64]{0:T(128)} %param.22) | copy-start | bytes 772
  18.8 23.4 %copy-start.21 = (f32[64]{0:T(128)S(1)}, f32[64]{0:T(128)}, u32[]{:S(2)}) copy-start(f32[64]{0:T(128)} %param.21) | copy-start | bytes 772
  20.5 9.1 %all-to-all-start.1 = ((bf16[128,2,512]{0,2,1:T(8,128)(2,1)}), bf16[128,2,512]{0,2,1:T(8,128)(2,1)S(1)}, u32[]{:S(2)}, u32[]{:S(2)}) async-start(bf16[128,2,512]{0,2,1:T(8,128)(2,1)} %bitcast.4), calls=%async_computation.1 | async-start | bytes 524288 | tf_op jit(solution)/shard_map/all_to_all | solution.py:79
  29.6 8.6 %all-to-all-start.2 = ((bf16[128,2,512]{0,2,1:T(8,128)(2,1)}), bf16[128,2,512]{0,2,1:T(8,128)(2,1)S(1)}, u32[]{:S(2)}, u32[]{:S(2)}) async-start(bf16[128,2,512]{0,2,1:T(8,128)(2,1)} %bitcast.7), calls=%async_computation.2 | async-start | bytes 524288 | tf_op jit(solution)/shard_map/all_to_all | solution.py:80
  38.2 27.6 %all-to-all-start = ((bf16[128,2,4096]{0,2,1:T(8,128)(2,1)}), bf16[128,2,4096]{0,2,1:T(8,128)(2,1)S(1)}, u32[]{:S(2)}, u32[]{:S(2)}) async-start(bf16[128,2,4096]{0,2,1:T(8,128)(2,1)} %bitcast.1), calls=%async_computation | async-start | bytes 4194304 | tf_op jit(solution)/shard_map/all_to_all | solution.py:77
  42.0 308.5 %all-gather.5.cloned.1.call-start = ((), (), s32[]{:S(2)}) async-start(), calls=%async_computation.6 | async-start | bytes 35651584 | tf_op jit(solution)/shard_map/all_gather | solution.py:21
  70.2 2.2 collective-permute-start
  78.5 9.0 %copy-start.1 = (bf16[256,4096]{1,0:T(8,128)(2,1)}, bf16[256,4096]{1,0:T(8,128)(2,1)S(1)}, u32[]{:S(2)}) copy-start(bf16[256,4096]{1,0:T(8,128)(2,1)S(1)} %multiply_convert_fusion.4) | copy-start | bytes 6291460
  92.9 2.0 copy-start.25
  92.9 2.0 copy-start.27
  94.9 2.4 copy-start.4
  97.3 6.4 %copy-start.14 = (f32[4096]{0:T(1024)S(1)}, f32[4096]{0:T(1024)}, u32[]{:S(2)}) copy-start(f32[4096]{0:T(1024)} %param.28) | copy-start | bytes 49156
  97.3 6.5 %copy-start.30 = (u32[32]{0:T(128)S(1)}, u32[32]{0:T(128)}, u32[]{:S(2)}) copy-start(u32[32]{0:T(128)} %constant.53) | copy-start | bytes 388
  97.3 7.7 %copy-start.26 = (f32[64]{0:T(128)S(1)}, f32[64]{0:T(128)}, u32[]{:S(2)}) copy-start(f32[64]{0:T(128)} %get-tuple-element.136) | copy-start | bytes 772
  97.3 45.5 %copy-start.22 = (f32[64]{0:T(128)S(1)}, f32[64]{0:T(128)}, u32[]{:S(2)}) copy-start(f32[64]{0:T(128)} %param.21) | copy-start | bytes 772
  98.8 44.8 %all-to-all-start.4 = ((bf16[128,2,4096]{2,0,1:T(8,128)(2,1)}), bf16[128,2,4096]{2,0,1:T(8,128)(2,1)}, u32[]{:S(2)}, u32[]{:S(2)}) async-start(bf16[128,2,4096]{2,0,1:T(8,128)(2,1)} %bitcast.115), calls=%async_computation.4 | async-start | bytes 4194304 | tf_op jit(solution)/shard_map/all_to_all | solution.py:78
  103.6 355.5 %reduce-scatter.2.cloned.1.call-start = ((), (), s32[]{:S(2)}) async-start(), calls=%async_computation.7 | async-start | bytes 3145728 | tf_op jit(solution)/shard_map/reduce_scatter | solution.py:153
  164.8 6.9 %copy-start.16 = (f32[1,1,512]{2,1,0:T(1,128)S(1)}, f32[1,1,512]{2,1,0:T(1,128)}, u32[]{:S(2)}) copy-start(f32[1,1,512]{2,1,0:T(1,128)} %get-tuple-element.144) | copy-start | bytes 6148
  164.8 6.9 %copy-start.17 = (f32[1,1,512]{2,1,0:T(1,128)S(1)}, f32[1,1,512]{2,1,0:T(1,128)}, u32[]{:S(2)}) copy-start(f32[1,1,512]{2,1,0:T(1,128)} %get-tuple-element.147) | copy-start | bytes 6148
  164.8 6.9 %copy-start.18 = (f32[1,1,512]{2,1,0:T(1,128)S(1)}, f32[1,1,512]{2,1,0:T(1,128)}, u32[]{:S(2)}) copy-start(f32[1,1,512]{2,1,0:T(1,128)} %get-tuple-element.148) | copy-start | bytes 6148
  164.8 6.9 %copy-start.19 = (f32[1,1,512]{2,1,0:T(1,128)S(1)}, f32[1,1,512]{2,1,0:T(1,128)}, u32[]{:S(2)}) copy-start(f32[1,1,512]{2,1,0:T(1,128)} %get-tuple-element.149) | copy-start | bytes 6148
  164.8 6.9 %copy-start.20 = (f32[1,512]{1,0:T(1,128)S(1)}, f32[1,512]{1,0:T(1,128)}, u32[]{:S(2)}) copy-start(f32[1,512]{1,0:T(1,128)} %get-tuple-element.152) | copy-start | bytes 6148
  350.5 31.9 %copy-start.24 = (f32[64]{0:T(128)S(1)}, f32[64]{0:T(128)}, u32[]{:S(2)}) copy-start(f32[64]{0:T(128)} %get-tuple-element.134) | copy-start | bytes 772
  385.2 2.2 copy-start.3
  385.2 2.2 copy-start.29
  400.2 6.5 %copy-start.7 = (f32[2,128,64]{1,2,0:T(8,128)S(1)}, f32[2,128,64]{1,2,0:T(8,128)}, u32[]{:S(2)}) copy-start(f32[2,128,64]{1,2,0:T(8,128)} %get-tuple-element.154) | copy-start | bytes 196612
  (8 other events, 10.7 us)
Sparse Core Ops, SparseCore 0:
  8.9 171.0 all-gather.6
  181.6 168.8 all-gather.4
  427.2 31.8 reduce-scatter.1
